TPU v7x, 32 devices: a whole 2x2x4 slice. The times are simulated.
32 devices in a mesh: grp: 8 (over y, x, core), tile: 4 (over z).
Axes of the slice: x: 2, y: 2, z: 4, core: 2. Of those that a mesh axis runs over, the one named last changes fastest.
Arguments:
- atm_flux: float32 [6, 32768], P(None, ('grp', 'tile')), may hold values from -6 to 6
- send_block: int32 [32, 4, 4], P(('grp', 'tile')), may hold values from 0 to 7
- send_count: int32 [32, 4], P(('grp', 'tile')), may hold values from 1 to 4, as said below
- recv_block: int32 [32, 4, 4], P(('grp', 'tile')), may hold values from 0 to 63
- recv_weight: bfloat16 [32, 4, 4, 128, 128], P(('grp', 'tile')), may hold values from -0.5 to 0.5
- sea_temp: float32 [256, 1024], P('grp', 'tile'), may hold values from -6 to 6
- ocean_mask: int32 [256, 1024], P('grp', 'tile'), may hold values 0 or 1
Outputs:
- heat_flux: float32 [256, 1024], P('grp', 'tile')
- stress_curl: float32 [256, 1024], P('grp', 'tile')
- atm_return: float32 [4, 32768], P(None, ('grp', 'tile'))
Inputs may be any that keep to these rules, and one draw needn't show every extreme that they name: `send_count`: in every draw a quarter of the tile indices, drawn from the seed, receive exactly 4 blocks from every device of their group; every other pair carries 1 to 2 blocks.
All inputs are finite; a program needn't handle non-finite values. No bound on the sum of `ocean_mask` on one device may be relied on, other than what follows from the above.
Results may differ from a plain program's by a relative error of at most 0.0003.
Values sent between devices are 32-bit elements; how exact they have to be, the bound alone decides.
A program may use at most 64 MiB of HBM per device.

v0:
```python
import jax
import jax.numpy as jnp
from jax import lax
from jax.sharding import PartitionSpec as P

precise = lax.Precision.HIGHEST


def extended(block, sides, width):
    for axis, dim in sides:
        count = lax.axis_size(axis)
        forward = [(i, i + 1) for i in range(count - 1)]
        forward.append((count - 1, 0))
        backward = [(target, source) for source, target in forward]
        low = lax.ppermute(
            lax.slice_in_dim(block, block.shape[dim] - width, None, axis=dim), axis, forward
        )
        high = lax.ppermute(lax.slice_in_dim(block, 0, width, axis=dim), axis, backward)
        block = jnp.concatenate([low, block, high], axis=dim)
    return block


def from_partner(value, axis, stride):
    return lax.ppermute(value, axis, [(i, i ^ 1 << stride) for i in range(lax.axis_size(axis))])


def bulk_formula(fields, surface_temp, ocean_mask):
    sea_share = ocean_mask.astype(jnp.float32)
    wind_u, wind_v, air_temp, air_vapor, short_down, long_down = [fields[k] for k in range(6)]
    wind_speed = jnp.sqrt(wind_u * wind_u + wind_v * wind_v + 0.5)
    stress_x = 0.8 * wind_speed * wind_u * sea_share
    stress_y = 0.8 * wind_speed * wind_v * sea_share
    sensible = 0.6 * wind_speed * (surface_temp - air_temp)
    latent = 0.7 * wind_speed * (jnp.exp(0.3 * surface_temp) - air_vapor)
    long_up = 0.4 * (1.0 + 0.2 * surface_temp) ** 4
    heat_flux = (0.94 * short_down + long_down - long_up - sensible - latent) * sea_share
    surface = jnp.stack([surface_temp, sensible, latent, long_up]) * sea_share[None]
    return (stress_x, stress_y, heat_flux, surface)


def per_device(atm_flux, send_block, send_count, recv_block, recv_weight, sea_temp, ocean_mask):
    tile_count = lax.axis_size("tile")
    field_count = atm_flux.shape[0]
    block_cells = recv_weight.shape[-1]
    slot_count = send_block.shape[2]
    atm_blocks = atm_flux.shape[1] // block_cells
    ocean_rows, ocean_cols = sea_temp.shape
    ocean_blocks = ocean_rows * ocean_cols // block_cells
    slot_range = jnp.arange(slot_count, dtype=jnp.int32)
    blocks = atm_flux.reshape(field_count, atm_blocks, block_cells)
    send_index = send_block[0]
    pair_count = send_count[0]
    live_slots = (slot_range[None, :] < pair_count[:, None]).astype(jnp.float32)
    chosen = jnp.take(blocks, send_index, axis=1) * live_slots[None, :, :, None]
    incoming = lax.all_to_all(chosen, "tile", split_axis=1, concat_axis=1, tiled=True)
    weight_wide = recv_weight[0].astype(jnp.float32)
    remapped = jnp.einsum("scij,fscj->fsci", weight_wide, incoming, precision=precise)
    dest_block = recv_block[0]
    onehot = (
        jnp.arange(ocean_blocks, dtype=jnp.int32)[:, None] == dest_block.reshape(-1)[None, :]
    ).astype(jnp.float32)
    landed = jnp.einsum(
        "ok,fkj->foj",
        onehot,
        remapped.reshape(field_count, tile_count * slot_count, block_cells),
        precision=precise,
    )
    fields = landed.reshape(field_count, ocean_rows, ocean_cols)
    stress_x, stress_y, heat_flux, surface = bulk_formula(fields, sea_temp, ocean_mask)
    sea_share = ocean_mask.astype(jnp.float32)
    padded = extended(jnp.stack([stress_x, stress_y]), (("grp", 1), ("tile", 2)), 1)
    mirror_row = stress_x[ocean_rows - 1]
    for bit_number in range(tile_count.bit_length() - 1):
        mirror_row = from_partner(mirror_row, "tile", bit_number)
    fold_values = -jnp.flip(mirror_row)
    group_index = lax.axis_index("grp")
    south_rim = jnp.where(group_index == 0, 0.0, padded[0, 0, 1:-1])
    north_rim = jnp.where(group_index == lax.axis_size("grp") - 1, fold_values, padded[0, -1, 1:-1])
    column_x = jnp.concatenate([south_rim[None], stress_x, north_rim[None]], axis=0)
    stress_curl = 0.5 * (padded[1, 1:-1, 2:] - padded[1, 1:-1, :-2]) - 0.5 * (
        column_x[2:] - column_x[:-2]
    )
    stress_curl = stress_curl * sea_share
    surface_blocks = surface.reshape(surface.shape[0], ocean_blocks, block_cells)
    chosen_back = jnp.take(surface_blocks, dest_block, axis=1)
    returned = jnp.einsum("scij,fsci->fscj", weight_wide, chosen_back, precision=precise)
    arrived = lax.all_to_all(returned, "tile", split_axis=1, concat_axis=1, tiled=True)
    arrived = arrived * live_slots[None, :, :, None]
    atm_onehot = (
        jnp.arange(atm_blocks, dtype=jnp.int32)[:, None] == send_index.reshape(-1)[None, :]
    ).astype(jnp.float32)
    atm_part = jnp.einsum(
        "ak,fkj->faj",
        atm_onehot,
        arrived.reshape(surface.shape[0], tile_count * slot_count, block_cells),
        precision=precise,
    )
    return (heat_flux, stress_curl, atm_part.reshape(surface.shape[0], atm_blocks * block_cells))


def solution(mesh):
    placed = (
        P(None, ("grp", "tile")),
        P(("grp", "tile"), None, None),
        P(("grp", "tile"), None),
        P(("grp", "tile"), None, None),
        P(("grp", "tile"), None, None, None, None),
        P("grp", "tile"),
        P("grp", "tile"),
    )
    return jax.shard_map(
        per_device,
        mesh=mesh,
        in_specs=placed,
        out_specs=(P("grp", "tile"), P("grp", "tile"), P(None, ("grp", "tile"))),
        check_vma=False,
    )
```

profile of v0, /device:TPU:0, one launch (start us, length us, event | category | flops | bytes accessed | tf_op | source)
XLA Modules:
  0.0 37.9 jit_solution(13872398486308174749)
XLA Ops:
  0.6 0.0 copy-start
  0.6 0.7 %compare_select_fusion.2 = s32[4,4,1]{1,0,2:T(4,128)S(1)} fusion(s32[1,4,4]{2,1,0:T(4,128)} %param.8), kind=kLoop, calls=%fused_computation.52 | loop fusion | flops 48 | bytes 128 | tf_op jit(solution)/shard_map/jit(_take)/jit(_where)/select_n | solution.py:54
  1.4 0.1 reshape.162
  1.5 0.0 copy-start.4
  1.5 0.0 copy-start.7
  1.5 0.7 %copy-done.4 = s32[1,4,4]{2,1,0:T(4,128)S(1)} copy-done((s32[1,4,4]{2,1,0:T(4,128)S(1)}, s32[1,4,4]{2,1,0:T(4,128)}, u32[]{:S(2)}) %copy-start.4) | copy-done | bytes 88
  2.2 0.0 copy-done.7
  2.2 0.1 fusion.25
  2.2 1.3 %gather_fusion = f32[16,6,128]{2,1,0:T(8,128)S(1)} fusion(f32[6,8,128]{2,0,1:T(8,128)} %bitcast.69, s32[1024]{0:T(1024)S(1)} %pad_clamp_fusion.1), kind=kCustom, calls=%fused_computation | custom fusion | bytes 98368 | tf_op jit(solution)/shard_map/jit(_take)/gather | solution.py:54
  3.6 0.7 %fusion.6 = f32[6,4,4,128]{3,2,0,1:T(4,128)} fusion(f32[4,4,6,128]{3,2,1,0:T(8,128)S(1)} %bitcast.65, f32[4,4]{1,0:T(4,128)S(1)} %get-tuple-element.21, pred[4,4]{1,0:T(4,128)(4,1)S(1)} %get-tuple-element.22), kind=kLoop, calls=%fused_computation.14 | loop fusion | flops 24576 | bytes 98384 | tf_op jit(solution)/shard_map/mul | solution.py:54
  4.3 6.5 %all-to-all-start = ((f32[6,4,4,128]{3,2,0,1:T(4,128)}), f32[6,4,4,128]{3,2,0,1:T(4,128)S(1)}, u32[]{:S(2)}, u32[]{:S(2)}) async-start(f32[6,4,4,128]{3,2,0,1:T(4,128)} %fusion.6), calls=%async_computation | async-start | bytes 98304 | tf_op jit(solution)/shard_map/all_to_all | solution.py:55
  10.7 0.0 copy-done.3
  10.7 0.1 eq.37
  10.8 0.1 eq.43
  10.9 0.0 copy-done.2
  11.0 0.7 %copy-done.1 = s32[32,256]{1,0:T(8,128)S(1)} copy-done((s32[32,256]{1,0:T(8,128)S(1)}, s32[32,256]{1,0:T(8,128)}, u32[]{:S(2)}) %copy-start.1) | copy-done | bytes 32792
  11.7 0.1 reshape.170
  11.8 4.7 %all-to-all-done = f32[6,4,4,128]{3,2,0,1:T(4,128)S(1)} async-done(((f32[6,4,4,128]{3,2,0,1:T(4,128)}), f32[6,4,4,128]{3,2,0,1:T(4,128)S(1)}, u32[]{:S(2)}, u32[]{:S(2)}) %all-to-all-start) | async-done | bytes 49184 | tf_op jit(solution)/shard_map/all_to_all | solution.py:55
  16.4 0.0 copy-done
  16.4 0.9 %fusion.1 = f32[4,4,6,128]{3,2,1,0:T(8,128)S(1)} fusion(bf16[1,4,4,128,128]{4,3,2,1,0:T(8,128)(2,1)S(1)} %copy-done, f32[6,4,4,128]{3,2,0,1:T(4,128)S(1)} %all-to-all-done), kind=kOutput, calls=%fused_computation.6 | convolution fusion | flops 18874368 | bytes 622592 | tf_op jit(solution)/shard_map/scij,fscj->fsci/dot_general | solution.py:57
  17.4 0.4 convolution_bitcast_fusion
  17.8 0.7 %multiply_bitcast_fusion = (f32[1,32,256]{2,1,0:T(8,128)S(1)}, f32[32,256]{1,0:T(8,128)S(1)}, f32[32,256]{1,0:T(8,128)}, f32[32,256]{1,0:T(8,128)S(1)}, f32[32,256]{1,0:T(8,128)S(1)}, /*index=5*/f32[32,256]{1,0:T(8,128)S(1)}) fusion(f32[32,256]{1,0:T(8,128)S(1)} %squeeze.40, s32[32,256]{1,0:T(8,128)S(1)} %copy-done.1, f32[32,256]{1,0:T(8,128)S(1)} %squeeze.39, ...), kind=kLoop, calls=%fused_computation.37 | loop fusion | flops 212992 | bytes 425984 | tf_op jit(solution)/shard_map/stack | solution.py:71
  18.5 0.1 collective-permute-start
  18.6 2.6 %collective-permute-start.1 = (f32[2,1,256]{2,1,0:T(1,128)S(1)}, f32[2,1,256]{2,1,0:T(1,128)S(1)}, u32[]{:S(2)}, u32[]{:S(2)}) collective-permute-start(f32[2,1,256]{2,1,0:T(1,128)S(1)} %get-tuple-element.18), channel_id=1, source_target_pairs={{4,0},{8,4},{12,8},{16,12},{20,16},{24,20},{28,24},{0,28},{5,1},{9... | collective-permute-start | bytes 6152 | tf_op jit(solution)/shard_map/ppermute | solution.py:18
  21.2 0.8 %collective-permute-start.4 = (f32[256]{0:T(256)S(1)}, f32[256]{0:T(256)S(1)}, u32[]{:S(2)}, u32[]{:S(2)}) collective-permute-start(f32[256]{0:T(256)S(1)} %bitcast.73), channel_id=1, source_target_pairs={{0,1},{1,0},{2,3},{3,2},{4,5},{5,4},{6,7},{7,6},{8,9},{9,8},{10,11... | collective-permute-start | bytes 3080 | tf_op jit(solution)/shard_map/ppermute | solution.py:24
  22.2 0.1 maximum_multiply_fusion
  22.3 0.6 %gather_fusion.1 = f32[16,4,128]{2,1,0:T(4,128)S(1)} fusion(f32[4,64,128]{2,0,1:T(4,128)S(1)} %maximum_multiply_fusion, s32[1024]{0:T(1024)S(1)} %pad_clamp_fusion), kind=kCustom, calls=%fused_computation.1 | custom fusion | bytes 65600 | tf_op jit(solution)/shard_map/jit(_take)/gather | solution.py:85
  22.9 1.2 %convolution_bitcast_fusion.1 = f32[4,4,4,128]{3,0,2,1:T(4,128)} fusion(bf16[1,4,4,128,128]{4,3,2,1,0:T(8,128)(2,1)S(1)} %copy-done, f32[4,4,4,128]{3,2,1,0:T(4,128)S(1)} %bitcast.68, pred[4,4]{1,0:T(4,128)(4,1)S(1)} %compare_and_fusion), kind=kOutput, calls=%fused_computation.3 | convolution fusion | flops 12591104 | bytes 589840 | tf_op jit(solution)/shard_map/scij,fsci->fscj/dot_general | solution.py:86
  24.1 3.3 %all-to-all-start.1 = ((f32[4,4,4,128]{3,0,2,1:T(4,128)}), f32[4,4,4,128]{3,0,2,1:T(4,128)S(1)}, u32[]{:S(2)}, u32[]{:S(2)}) async-start(f32[4,4,4,128]{3,0,2,1:T(4,128)} %convolution_bitcast_fusion.1), calls=%async_computation.1 | async-start | bytes 65536 | tf_op jit(solution)/shard_map/all_to_all | solution.py:87
  27.4 0.0 collective-permute-done.4
  27.4 2.9 %collective-permute-start.5 = (f32[256]{0:T(256)S(1)}, f32[256]{0:T(256)S(1)}, u32[]{:S(2)}, u32[]{:S(2)}) collective-permute-start(f32[256]{0:T(256)S(1)} %collective-permute-done.4), channel_id=1, source_target_pairs={{0,2},{1,3},{2,0},{3,1},{4,6},{5,7},{6,4},{7,5},{8,10},{9,11},{10,... | collective-permute-start | bytes 3080 | tf_op jit(solution)/shard_map/ppermute | solution.py:24
  30.3 0.0 collective-permute-done
  30.3 0.0 collective-permute-done.1
  30.3 0.1 fusion.29
  30.4 1.5 %collective-permute-start.3 = (f32[2,34,1]{2,1,0:T(8,128)S(1)}, f32[2,34,1]{2,1,0:T(8,128)S(1)}, u32[]{:S(2)}, u32[]{:S(2)}) collective-permute-start(f32[2,34,1]{2,1,0:T(8,128)S(1)} %get-tuple-element.17), channel_id=1, source_target_pairs={{0,1},{1,2},{2,3},{3,0},{4,5},{5,6},{6,7},{7,4},{8,9},{9,10},{10,1... | collective-permute-start | bytes 824 | tf_op jit(solution)/shard_map/ppermute | solution.py:15
  31.9 2.4 %collective-permute-start.2 = (f32[2,34,1]{2,1,0:T(8,128)S(1)}, f32[2,34,1]{2,1,0:T(8,128)S(1)}, u32[]{:S(2)}, u32[]{:S(2)}) collective-permute-start(f32[2,34,1]{2,1,0:T(8,128)S(1)} %get-tuple-element.16), channel_id=1, source_target_pairs={{1,0},{2,1},{3,2},{0,3},{5,4},{6,5},{7,6},{4,7},{9,8},{10,9},{11,1... | collective-permute-start | bytes 824 | tf_op jit(solution)/shard_map/ppermute | solution.py:18
  34.2 0.0 copy-done.5
  34.2 0.0 collective-permute-done.5
  34.2 0.1 rev.4
  34.3 0.7 %slice-done = f32[1,1,256]{2,1,0:T(1,128)S(1)} async-done(((f32[2,1,256]{2,1,0:T(1,128)}), f32[1,1,256]{2,1,0:T(1,128)S(1)}, s32[]{:S(2)}) %slice-start) | async-done | bytes 1048 | tf_op jit(solution)/shard_map/slice | solution.py:78
  35.0 1.3 %collective-permute-done.3 = f32[2,34,1]{2,1,0:T(8,128)S(1)} collective-permute-done((f32[2,34,1]{2,1,0:T(8,128)S(1)}, f32[2,34,1]{2,1,0:T(8,128)S(1)}, u32[]{:S(2)}, u32[]{:S(2)}) %collective-permute-start.3) | collective-permute-done | bytes 304 | tf_op jit(solution)/shard_map/ppermute | solution.py:15
  36.3 0.0 collective-permute-done.2
  36.3 0.0 copy-done.6
  36.3 0.7 %fusion.10 = f32[32,256]{1,0:T(8,128)} fusion(f32[32,256]{1,0:T(8,128)S(1)} %get-tuple-element.12, f32[1,256]{1,0:T(1,128)S(1)} %fusion.26, f32[1,256]{1,0:T(1,128)S(1)} %bitcast.72, f32[2,34,1]{2,1,0:T(8,128)S(1)} %collective-permute-done.3, f32[2,1,256]{2,1,0:T(1,128)S(1)} %copy-done.6, f32[2,1,256]{2,1,0:T(1,128)S(1)} %collective-permute-done, ...), kind=kLoop, calls=%fused_computation.19 | loop fusion | flops 139264 | bytes 170528 | tf_op jit(solution)/shard_map/mul | solution.py:83
  37.0 0.0 all-to-all-done.1
  37.0 0.1 broadcast_multiply_fusion
  37.1 0.1 convolution_bitcast_fusion.2
  37.2 0.6 %copy.32 = f32[1,4,8,128]{3,1,2,0:T(4,128)} copy(f32[1,4,8,128]{3,2,1,0:T(8,128)S(1)} %convolution_bitcast_fusion.2) | data formatting | bytes 32768
  (27 shorter events, 0.3 us)
Async XLA Ops:
  0.6 15.8 %copy-start = (bf16[1,4,4,128,128]{4,3,2,1,0:T(8,128)(2,1)S(1)}, bf16[1,4,4,128,128]{4,3,2,1,0:T(8,128)(2,1)}, u32[]{:S(2)}) copy-start(bf16[1,4,4,128,128]{4,3,2,1,0:T(8,128)(2,1)} %param.11) | copy-start | bytes 1572868
  1.5 0.7 %copy-start.4 = (s32[1,4,4]{2,1,0:T(4,128)S(1)}, s32[1,4,4]{2,1,0:T(4,128)}, u32[]{:S(2)}) copy-start(s32[1,4,4]{2,1,0:T(4,128)} %param.8) | copy-start | bytes 196
  1.5 0.7 %copy-start.7 = (s32[1,4]{1,0:T(1,128)S(1)}, s32[1,4]{1,0:T(1,128)}, u32[]{:S(2)}) copy-start(s32[1,4]{1,0:T(1,128)} %param.9) | copy-start | bytes 52
  4.3 6.5 %copy-start.3 = (s32[1,4,4]{2,1,0:T(4,128)S(1)}, s32[1,4,4]{2,1,0:T(4,128)}, u32[]{:S(2)}) copy-start(s32[1,4,4]{2,1,0:T(4,128)} %param.10) | copy-start | bytes 196
  4.3 6.7 %copy-start.2 = (f32[32,256]{1,0:T(8,128)S(1)}, f32[32,256]{1,0:T(8,128)}, u32[]{:S(2)}) copy-start(f32[32,256]{1,0:T(8,128)} %param.12) | copy-start | bytes 98308
  4.3 12.2 %all-to-all-start = ((f32[6,4,4,128]{3,2,0,1:T(4,128)}), f32[6,4,4,128]{3,2,0,1:T(4,128)S(1)}, u32[]{:S(2)}, u32[]{:S(2)}) async-start(f32[6,4,4,128]{3,2,0,1:T(4,128)} %fusion.6), calls=%async_computation | async-start | bytes 98304 | tf_op jit(solution)/shard_map/all_to_all | solution.py:55
  10.9 0.8 %copy-start.1 = (s32[32,256]{1,0:T(8,128)S(1)}, s32[32,256]{1,0:T(8,128)}, u32[]{:S(2)}) copy-start(s32[32,256]{1,0:T(8,128)} %param.13) | copy-start | bytes 98308
  18.5 11.7 %collective-permute-start = (f32[2,1,256]{2,1,0:T(1,128)S(1)}, f32[2,1,256]{2,1,0:T(1,128)S(1)}, u32[]{:S(2)}, u32[]{:S(2)}) collective-permute-start(f32[2,1,256]{2,1,0:T(1,128)S(1)} %get-tuple-element.19), channel_id=1, source_target_pairs={{0,4},{4,8},{8,12},{12,16},{16,20},{20,24},{24,28},{28,0},{1,5},{5... | collective-permute-start | bytes 6152 | tf_op jit(solution)/shard_map/ppermute | solution.py:15
  18.6 11.7 %collective-permute-start.1 = (f32[2,1,256]{2,1,0:T(1,128)S(1)}, f32[2,1,256]{2,1,0:T(1,128)S(1)}, u32[]{:S(2)}, u32[]{:S(2)}) collective-permute-start(f32[2,1,256]{2,1,0:T(1,128)S(1)} %get-tuple-element.18), channel_id=1, source_target_pairs={{4,0},{8,4},{12,8},{16,12},{20,16},{24,20},{28,24},{0,28},{5,1},{9... | collective-permute-start | bytes 6152 | tf_op jit(solution)/shard_map/ppermute | solution.py:18
  21.2 6.2 %collective-permute-start.4 = (f32[256]{0:T(256)S(1)}, f32[256]{0:T(256)S(1)}, u32[]{:S(2)}, u32[]{:S(2)}) collective-permute-start(f32[256]{0:T(256)S(1)} %bitcast.73), channel_id=1, source_target_pairs={{0,1},{1,0},{2,3},{3,2},{4,5},{5,4},{6,7},{7,6},{8,9},{9,8},{10,11... | collective-permute-start | bytes 3080 | tf_op jit(solution)/shard_map/ppermute | solution.py:24
  24.1 12.9 %all-to-all-start.1 = ((f32[4,4,4,128]{3,0,2,1:T(4,128)}), f32[4,4,4,128]{3,0,2,1:T(4,128)S(1)}, u32[]{:S(2)}, u32[]{:S(2)}) async-start(f32[4,4,4,128]{3,0,2,1:T(4,128)} %convolution_bitcast_fusion.1), calls=%async_computation.1 | async-start | bytes 65536 | tf_op jit(solution)/shard_map/all_to_all | solution.py:87
  27.4 6.8 %collective-permute-start.5 = (f32[256]{0:T(256)S(1)}, f32[256]{0:T(256)S(1)}, u32[]{:S(2)}, u32[]{:S(2)}) collective-permute-start(f32[256]{0:T(256)S(1)} %collective-permute-done.4), channel_id=1, source_target_pairs={{0,2},{1,3},{2,0},{3,1},{4,6},{5,7},{6,4},{7,5},{8,10},{9,11},{10,... | collective-permute-start | bytes 3080 | tf_op jit(solution)/shard_map/ppermute | solution.py:24
  30.3 3.9 %copy-start.5 = (f32[2,1,256]{2,1,0:T(1,128)}, f32[2,1,256]{2,1,0:T(1,128)S(1)}, u32[]{:S(2)}) copy-start(f32[2,1,256]{2,1,0:T(1,128)S(1)} %collective-permute-done.1) | copy-start | bytes 6148
  30.4 5.9 %collective-permute-start.3 = (f32[2,34,1]{2,1,0:T(8,128)S(1)}, f32[2,34,1]{2,1,0:T(8,128)S(1)}, u32[]{:S(2)}, u32[]{:S(2)}) collective-permute-start(f32[2,34,1]{2,1,0:T(8,128)S(1)} %get-tuple-element.17), channel_id=1, source_target_pairs={{0,1},{1,2},{2,3},{3,0},{4,5},{5,6},{6,7},{7,4},{8,9},{9,10},{10,1... | collective-permute-start | bytes 824 | tf_op jit(solution)/shard_map/ppermute | solution.py:15
  31.9 4.4 %collective-permute-start.2 = (f32[2,34,1]{2,1,0:T(8,128)S(1)}, f32[2,34,1]{2,1,0:T(8,128)S(1)}, u32[]{:S(2)}, u32[]{:S(2)}) collective-permute-start(f32[2,34,1]{2,1,0:T(8,128)S(1)} %get-tuple-element.16), channel_id=1, source_target_pairs={{1,0},{2,1},{3,2},{0,3},{5,4},{6,5},{7,6},{4,7},{9,8},{10,9},{11,1... | collective-permute-start | bytes 824 | tf_op jit(solution)/shard_map/ppermute | solution.py:18
  34.3 0.7 %slice-start = ((f32[2,1,256]{2,1,0:T(1,128)}), f32[1,1,256]{2,1,0:T(1,128)S(1)}, s32[]{:S(2)}) async-start(f32[2,1,256]{2,1,0:T(1,128)} %copy-done.5), calls=%async_computation.2 | async-start | bytes 2048 | tf_op jit(solution)/shard_map/slice | solution.py:78
  35.0 1.3 %copy-start.6 = (f32[2,1,256]{2,1,0:T(1,128)S(1)}, f32[2,1,256]{2,1,0:T(1,128)}, u32[]{:S(2)}) copy-start(f32[2,1,256]{2,1,0:T(1,128)} %copy-done.5) | copy-start | bytes 6148
where the time goes:
time: 38.4 us; the launch traced here: 37.9 us
  starting transfers between devices  20 us (52%)
  waiting for transfers between devices  5.95 us (15%)
  local copies, waits for them, and re-layouts  5.32 us (14%)
  other arithmetic  3.19 us (8%)
  matrix products  2.61 us (7%)
  between operations  0.82 us (2%)
    all_to_all x1, starting transfers between devices, per_device(): lax.all_to_all(chosen, 'tile', split_axis=1, concat_axis=1, tiled=True)  6.48 us
    ppermute x2, starting transfers between devices, extended(): lax.ppermute(lax.slice_in_dim(block, 0, width, axis=dim), axis, backward)  4.99 us
    all_to_all x1, waiting for transfers between devices, per_device(): lax.all_to_all(chosen, 'tile', split_axis=1, concat_axis=1, tiled=True)  4.65 us
    ppermute x2, starting transfers between devices, from_partner(): lax.ppermute(value, axis, [(i, i ^ 1 << stride) for i in range(lax.axis_s...  3.71 us
    all_to_all x1, starting transfers between devices, per_device(): lax.all_to_all(returned, 'tile', split_axis=1, concat_axis=1, tiled=True)  3.26 us
    unnamed x17, local copies, waits for them, and re-layouts  2.03 us
    ppermute x2, starting transfers between devices, extended(): lax.ppermute(lax.slice_in_dim(block, block.shape[dim] - width, None, axis...  1.53 us
    gather x1, local copies, waits for them, and re-layouts, per_device(): chosen = jnp.take(blocks, send_index, axis=1) * live_slots[None, :, :, None]  1.31 us
  transfers between devices with their start and end apart: 8, of which 2 were waited for; matrix products, arithmetic and copies ran while one was open for 9% of the time, Pallas kernels for 0%

commit v1 on v0

--- a/solution.py
+++ b/solution.py
@@ -84,7 +84,10 @@
     surface_blocks = surface.reshape(surface.shape[0], ocean_blocks, block_cells)
     chosen_back = jnp.take(surface_blocks, dest_block, axis=1)
     returned = jnp.einsum("scij,fsci->fscj", weight_wide, chosen_back, precision=precise)
-    arrived = lax.all_to_all(returned, "tile", split_axis=1, concat_axis=1, tiled=True)
+    size = lax.axis_size("tile")
+    pieces = jnp.stack(jnp.split(returned, size, axis=1), axis=0)
+    pieces = lax.all_to_all(pieces, "tile", split_axis=0, concat_axis=0)
+    arrived = jnp.concatenate(pieces, axis=1)
     arrived = arrived * live_slots[None, :, :, None]
     atm_onehot = (
         jnp.arange(atm_blocks, dtype=jnp.int32)[:, None] == send_index.reshape(-1)[None, :]

time: 38.4 us -> 38.3 us (level)
  matrix products: 2.61 us -> 2.05 us
  other arithmetic: 3.19 us -> 3.73 us
    dot_general x1, matrix products: 1.2 us -> 0.57 us  [per_device(): jnp.einsum('scij,fsci->fscj', weight_wide, chosen_back, precision=precise)]
    another operation x0 -> x1, other arithmetic: none -> 0.62 us  [per_device(): pieces = jnp.stack(jnp.split(returned, size, axis=1), axis=0)]
where the time goes in v1:
time: 38.3 us; the launch traced here: 37.8 us
  starting transfers between devices  20 us (52%)
  waiting for transfers between devices  5.87 us (15%)
  local copies, waits for them, and re-layouts  5.4 us (14%)
  other arithmetic  3.73 us (10%)
  matrix products  2.05 us (5%)
  between operations  0.81 us (2%)
    all_to_all x1, starting transfers between devices, per_device(): lax.all_to_all(chosen, 'tile', split_axis=1, concat_axis=1, tiled=True)  6.48 us
    ppermute x2, starting transfers between devices, extended(): lax.ppermute(lax.slice_in_dim(block, 0, width, axis=dim), axis, backward)  4.99 us
    all_to_all x1, waiting for transfers between devices, per_device(): lax.all_to_all(chosen, 'tile', split_axis=1, concat_axis=1, tiled=True)  4.57 us
    ppermute x2, starting transfers between devices, from_partner(): lax.ppermute(value, axis, [(i, i ^ 1 << stride) for i in range(lax.axis_s...  3.71 us
    all_to_all x1, starting transfers between devices, per_device(): pieces = lax.all_to_all(pieces, 'tile', split_axis=0, concat_axis=0)  3.26 us
    unnamed x17, local copies, waits for them, and re-layouts  2.03 us
    ppermute x2, starting transfers between devices, extended(): lax.ppermute(lax.slice_in_dim(block, block.shape[dim] - width, None, axis...  1.53 us
    gather x1, local copies, waits for them, and re-layouts, per_device(): chosen = jnp.take(blocks, send_index, axis=1) * live_slots[None, :, :, None]  1.31 us
  transfers between devices with their start and end apart: 8, of which 2 were waited for; matrix products, arithmetic and copies ran while one was open for 9% of the time, Pallas kernels for 0%

profile of v1, /device:TPU:0, one launch (start us, length us, event | category | flops | bytes accessed | tf_op | source)
XLA Modules:
  0.0 37.8 jit_solution(5915072367134180304)
XLA Ops:
  0.6 0.0 copy-start
  0.6 0.7 %compare_select_fusion.2 = s32[4,4,1]{1,0,2:T(4,128)S(1)} fusion(s32[1,4,4]{2,1,0:T(4,128)} %param.8), kind=kLoop, calls=%fused_computation.57 | loop fusion | flops 48 | bytes 128 | tf_op jit(solution)/shard_map/jit(_take)/jit(_where)/select_n | solution.py:54
  1.4 0.1 reshape.178
  1.5 0.0 copy-start.7
  1.5 0.7 %copy-done.4 = s32[1,4,4]{2,1,0:T(4,128)S(1)} copy-done((s32[1,4,4]{2,1,0:T(4,128)S(1)}, s32[1,4,4]{2,1,0:T(4,128)}, u32[]{:S(2)}) %copy-start.4) | copy-done | bytes 88
  2.2 0.0 copy-done.7
  2.2 0.1 fusion.25
  2.2 1.3 %gather_fusion = f32[16,6,128]{2,1,0:T(8,128)S(1)} fusion(f32[6,8,128]{2,0,1:T(8,128)} %bitcast.78, s32[1024]{0:T(1024)S(1)} %pad_clamp_fusion.1), kind=kCustom, calls=%fused_computation | custom fusion | bytes 98368 | tf_op jit(solution)/shard_map/jit(_take)/gather | solution.py:54
  3.6 0.7 %fusion.6 = f32[6,4,4,128]{3,2,0,1:T(4,128)} fusion(f32[4,4,6,128]{3,2,1,0:T(8,128)S(1)} %bitcast.75, f32[4,4]{1,0:T(4,128)S(1)} %get-tuple-element.25, pred[4,4]{1,0:T(4,128)(4,1)S(1)} %get-tuple-element.26), kind=kLoop, calls=%fused_computation.14 | loop fusion | flops 24576 | bytes 98384 | tf_op jit(solution)/shard_map/mul | solution.py:54
  4.3 6.5 %all-to-all-start = ((f32[6,4,4,128]{3,2,0,1:T(4,128)}), f32[6,4,4,128]{3,2,0,1:T(4,128)S(1)}, u32[]{:S(2)}, u32[]{:S(2)}) async-start(f32[6,4,4,128]{3,2,0,1:T(4,128)} %fusion.6), calls=%async_computation | async-start | bytes 98304 | tf_op jit(solution)/shard_map/all_to_all | solution.py:55
  10.7 0.0 copy-done.3
  10.7 0.1 eq.37
  10.8 0.1 reshape.175
  10.9 0.1 eq.43
  11.0 0.0 copy-done.2
  11.0 0.7 %copy-done.1 = s32[32,256]{1,0:T(8,128)S(1)} copy-done((s32[32,256]{1,0:T(8,128)S(1)}, s32[32,256]{1,0:T(8,128)}, u32[]{:S(2)}) %copy-start.1) | copy-done | bytes 32792
  11.8 0.1 reshape.186
  11.9 4.6 %all-to-all-done = f32[6,4,4,128]{3,2,0,1:T(4,128)S(1)} async-done(((f32[6,4,4,128]{3,2,0,1:T(4,128)}), f32[6,4,4,128]{3,2,0,1:T(4,128)S(1)}, u32[]{:S(2)}, u32[]{:S(2)}) %all-to-all-start) | async-done | bytes 49184 | tf_op jit(solution)/shard_map/all_to_all | solution.py:55
  16.4 0.0 copy-done
  16.4 0.9 %fusion.1 = f32[4,4,6,128]{3,2,1,0:T(8,128)S(1)} fusion(bf16[1,4,4,128,128]{4,3,2,1,0:T(8,128)(2,1)S(1)} %copy-done, f32[6,4,4,128]{3,2,0,1:T(4,128)S(1)} %all-to-all-done), kind=kOutput, calls=%fused_computation.6 | convolution fusion | flops 18874368 | bytes 622592 | tf_op jit(solution)/shard_map/scij,fscj->fsci/dot_general | solution.py:57
  17.3 0.4 convolution_bitcast_fusion
  17.8 0.7 %multiply_bitcast_fusion = (f32[1,32,256]{2,1,0:T(8,128)S(1)}, f32[32,256]{1,0:T(8,128)S(1)}, f32[32,256]{1,0:T(8,128)}, f32[32,256]{1,0:T(8,128)S(1)}, f32[32,256]{1,0:T(8,128)S(1)}, /*index=5*/f32[32,256]{1,0:T(8,128)S(1)}) fusion(f32[32,256]{1,0:T(8,128)S(1)} %squeeze.40, s32[32,256]{1,0:T(8,128)S(1)} %copy-done.1, f32[32,256]{1,0:T(8,128)S(1)} %squeeze.39, ...), kind=kLoop, calls=%fused_computation.38 | loop fusion | flops 212992 | bytes 425984 | tf_op jit(solution)/shard_map/stack | solution.py:71
  18.5 0.1 collective-permute-start
  18.6 2.6 %collective-permute-start.1 = (f32[2,1,256]{2,1,0:T(1,128)S(1)}, f32[2,1,256]{2,1,0:T(1,128)S(1)}, u32[]{:S(2)}, u32[]{:S(2)}) collective-permute-start(f32[2,1,256]{2,1,0:T(1,128)S(1)} %get-tuple-element.18), channel_id=1, source_target_pairs={{4,0},{8,4},{12,8},{16,12},{20,16},{24,20},{28,24},{0,28},{5,1},{9... | collective-permute-start | bytes 6152 | tf_op jit(solution)/shard_map/ppermute | solution.py:18
  21.2 0.8 %collective-permute-start.4 = (f32[256]{0:T(256)S(1)}, f32[256]{0:T(256)S(1)}, u32[]{:S(2)}, u32[]{:S(2)}) collective-permute-start(f32[256]{0:T(256)S(1)} %bitcast.83), channel_id=1, source_target_pairs={{0,1},{1,0},{2,3},{3,2},{4,5},{5,4},{6,7},{7,6},{8,9},{9,8},{10,11... | collective-permute-start | bytes 3080 | tf_op jit(solution)/shard_map/ppermute | solution.py:24
  22.2 0.1 maximum_multiply_fusion
  22.3 0.6 %gather_fusion.1 = f32[16,4,128]{2,1,0:T(4,128)S(1)} fusion(f32[4,64,128]{2,0,1:T(4,128)S(1)} %maximum_multiply_fusion, s32[1024]{0:T(1024)S(1)} %pad_clamp_fusion), kind=kCustom, calls=%fused_computation.1 | custom fusion | bytes 65600 | tf_op jit(solution)/shard_map/jit(_take)/gather | solution.py:85
  22.9 0.6 %convolution_bitcast_fusion.1 = f32[4,4,4,128]{3,0,2,1:T(4,128)S(1)} fusion(bf16[1,4,4,128,128]{4,3,2,1,0:T(8,128)(2,1)S(1)} %copy-done, f32[4,4,4,128]{3,2,1,0:T(4,128)S(1)} %bitcast.77, pred[4,4]{1,0:T(4,128)(4,1)S(1)} %compare_and_fusion), kind=kOutput, calls=%fused_computation.3 | convolution fusion | flops 12591104 | bytes 589840 | tf_op jit(solution)/shard_map/scij,fsci->fscj/dot_general | solution.py:86
  23.5 0.6 %pad_maximum_fusion.11 = f32[4,4,1,4,128]{4,1,3,2,0:T(4,128)} fusion(f32[1,4,1,4,128]{4,1,3,2,0:T(4,128)S(1)} %get-tuple-element.22, f32[1,4,1,4,128]{4,1,3,2,0:T(4,128)S(1)} %get-tuple-element.23, f32[1,4,1,4,128]{4,1,3,2,0:T(4,128)S(1)} %get-tuple-element.24, f32[1,4,1,4,128]{4,1,3,2,0:T(4,128)S(1)} %get-tuple-element.21), kind=kLoop, calls=%fused_computation.34 | loop fusion | flops 24576 | bytes 65536 | tf_op jit(solution)/shard_map/stack | solution.py:88
  24.1 3.3 %all-to-all-start.1 = ((f32[4,4,1,4,128]{4,1,3,2,0:T(4,128)}), f32[4,4,1,4,128]{4,1,3,2,0:T(4,128)S(1)}, u32[]{:S(2)}, u32[]{:S(2)}) async-start(f32[4,4,1,4,128]{4,1,3,2,0:T(4,128)} %pad_maximum_fusion.11), calls=%async_computation.1 | async-start | bytes 65536 | tf_op jit(solution)/shard_map/all_to_all | solution.py:89
  27.4 0.0 collective-permute-done.4
  27.4 2.9 %collective-permute-start.5 = (f32[256]{0:T(256)S(1)}, f32[256]{0:T(256)S(1)}, u32[]{:S(2)}, u32[]{:S(2)}) collective-permute-start(f32[256]{0:T(256)S(1)} %collective-permute-done.4), channel_id=1, source_target_pairs={{0,2},{1,3},{2,0},{3,1},{4,6},{5,7},{6,4},{7,5},{8,10},{9,11},{10,... | collective-permute-start | bytes 3080 | tf_op jit(solution)/shard_map/ppermute | solution.py:24
  30.3 0.0 collective-permute-done
  30.3 0.0 collective-permute-done.1
  30.3 0.1 fusion.29
  30.4 1.5 %collective-permute-start.3 = (f32[2,34,1]{2,1,0:T(8,128)S(1)}, f32[2,34,1]{2,1,0:T(8,128)S(1)}, u32[]{:S(2)}, u32[]{:S(2)}) collective-permute-start(f32[2,34,1]{2,1,0:T(8,128)S(1)} %get-tuple-element.17), channel_id=1, source_target_pairs={{0,1},{1,2},{2,3},{3,0},{4,5},{5,6},{6,7},{7,4},{8,9},{9,10},{10,1... | collective-permute-start | bytes 824 | tf_op jit(solution)/shard_map/ppermute | solution.py:15
  31.8 2.4 %collective-permute-start.2 = (f32[2,34,1]{2,1,0:T(8,128)S(1)}, f32[2,34,1]{2,1,0:T(8,128)S(1)}, u32[]{:S(2)}, u32[]{:S(2)}) collective-permute-start(f32[2,34,1]{2,1,0:T(8,128)S(1)} %get-tuple-element.16), channel_id=1, source_target_pairs={{1,0},{2,1},{3,2},{0,3},{5,4},{6,5},{7,6},{4,7},{9,8},{10,9},{11,1... | collective-permute-start | bytes 824 | tf_op jit(solution)/shard_map/ppermute | solution.py:18
  34.2 0.0 copy-done.5
  34.2 0.0 collective-permute-done.5
  34.2 0.1 rev.4
  34.3 0.7 %slice-done = f32[1,1,256]{2,1,0:T(1,128)S(1)} async-done(((f32[2,1,256]{2,1,0:T(1,128)}), f32[1,1,256]{2,1,0:T(1,128)S(1)}, s32[]{:S(2)}) %slice-start) | async-done | bytes 1048 | tf_op jit(solution)/shard_map/slice | solution.py:78
  35.0 1.3 %collective-permute-done.3 = f32[2,34,1]{2,1,0:T(8,128)S(1)} collective-permute-done((f32[2,34,1]{2,1,0:T(8,128)S(1)}, f32[2,34,1]{2,1,0:T(8,128)S(1)}, u32[]{:S(2)}, u32[]{:S(2)}) %collective-permute-start.3) | collective-permute-done | bytes 304 | tf_op jit(solution)/shard_map/ppermute | solution.py:15
  36.3 0.0 collective-permute-done.2
  36.3 0.0 copy-done.6
  36.3 0.7 %fusion.10 = f32[32,256]{1,0:T(8,128)} fusion(f32[32,256]{1,0:T(8,128)S(1)} %get-tuple-element.12, f32[1,256]{1,0:T(1,128)S(1)} %fusion.26, f32[1,256]{1,0:T(1,128)S(1)} %bitcast.82, f32[2,34,1]{2,1,0:T(8,128)S(1)} %collective-permute-done.3, f32[2,1,256]{2,1,0:T(1,128)S(1)} %copy-done.6, f32[2,1,256]{2,1,0:T(1,128)S(1)} %collective-permute-done, ...), kind=kLoop, calls=%fused_computation.19 | loop fusion | flops 139264 | bytes 170528 | tf_op jit(solution)/shard_map/mul | solution.py:83
  37.0 0.0 all-to-all-done.1
  37.0 0.2 convolution_bitcast_fusion.2
  37.2 0.6 %copy.32 = f32[1,4,8,128]{3,1,2,0:T(4,128)} copy(f32[1,4,8,128]{3,2,1,0:T(8,128)S(1)} %convolution_bitcast_fusion.2) | data formatting | bytes 32768
  (29 shorter events, 0.3 us)
Async XLA Ops:
  0.6 15.8 %copy-start = (bf16[1,4,4,128,128]{4,3,2,1,0:T(8,128)(2,1)S(1)}, bf16[1,4,4,128,128]{4,3,2,1,0:T(8,128)(2,1)}, u32[]{:S(2)}) copy-start(bf16[1,4,4,128,128]{4,3,2,1,0:T(8,128)(2,1)} %param.11) | copy-start | bytes 1572868
  1.5 0.7 %copy-start.4 = (s32[1,4,4]{2,1,0:T(4,128)S(1)}, s32[1,4,4]{2,1,0:T(4,128)}, u32[]{:S(2)}) copy-start(s32[1,4,4]{2,1,0:T(4,128)} %param.8) | copy-start | bytes 196
  1.5 0.7 %copy-start.7 = (s32[1,4]{1,0:T(1,128)S(1)}, s32[1,4]{1,0:T(1,128)}, u32[]{:S(2)}) copy-start(s32[1,4]{1,0:T(1,128)} %param.9) | copy-start | bytes 52
  4.3 6.5 %copy-start.3 = (s32[1,4,4]{2,1,0:T(4,128)S(1)}, s32[1,4,4]{2,1,0:T(4,128)}, u32[]{:S(2)}) copy-start(s32[1,4,4]{2,1,0:T(4,128)} %param.10) | copy-start | bytes 196
  4.3 6.7 %copy-start.2 = (f32[32,256]{1,0:T(8,128)S(1)}, f32[32,256]{1,0:T(8,128)}, u32[]{:S(2)}) copy-start(f32[32,256]{1,0:T(8,128)} %param.12) | copy-start | bytes 98308
  4.3 12.2 %all-to-all-start = ((f32[6,4,4,128]{3,2,0,1:T(4,128)}), f32[6,4,4,128]{3,2,0,1:T(4,128)S(1)}, u32[]{:S(2)}, u32[]{:S(2)}) async-start(f32[6,4,4,128]{3,2,0,1:T(4,128)} %fusion.6), calls=%async_computation | async-start | bytes 98304 | tf_op jit(solution)/shard_map/all_to_all | solution.py:55
  11.0 0.8 %copy-start.1 = (s32[32,256]{1,0:T(8,128)S(1)}, s32[32,256]{1,0:T(8,128)}, u32[]{:S(2)}) copy-start(s32[32,256]{1,0:T(8,128)} %param.13) | copy-start | bytes 98308
  18.5 11.7 %collective-permute-start = (f32[2,1,256]{2,1,0:T(1,128)S(1)}, f32[2,1,256]{2,1,0:T(1,128)S(1)}, u32[]{:S(2)}, u32[]{:S(2)}) collective-permute-start(f32[2,1,256]{2,1,0:T(1,128)S(1)} %get-tuple-element.19), channel_id=1, source_target_pairs={{0,4},{4,8},{8,12},{12,16},{16,20},{20,24},{24,28},{28,0},{1,5},{5... | collective-permute-start | bytes 6152 | tf_op jit(solution)/shard_map/ppermute | solution.py:15
  18.6 11.7 %collective-permute-start.1 = (f32[2,1,256]{2,1,0:T(1,128)S(1)}, f32[2,1,256]{2,1,0:T(1,128)S(1)}, u32[]{:S(2)}, u32[]{:S(2)}) collective-permute-start(f32[2,1,256]{2,1,0:T(1,128)S(1)} %get-tuple-element.18), channel_id=1, source_target_pairs={{4,0},{8,4},{12,8},{16,12},{20,16},{24,20},{28,24},{0,28},{5,1},{9... | collective-permute-start | bytes 6152 | tf_op jit(solution)/shard_map/ppermute | solution.py:18
  21.2 6.2 %collective-permute-start.4 = (f32[256]{0:T(256)S(1)}, f32[256]{0:T(256)S(1)}, u32[]{:S(2)}, u32[]{:S(2)}) collective-permute-start(f32[256]{0:T(256)S(1)} %bitcast.83), channel_id=1, source_target_pairs={{0,1},{1,0},{2,3},{3,2},{4,5},{5,4},{6,7},{7,6},{8,9},{9,8},{10,11... | collective-permute-start | bytes 3080 | tf_op jit(solution)/shard_map/ppermute | solution.py:24
  24.1 12.9 %all-to-all-start.1 = ((f32[4,4,1,4,128]{4,1,3,2,0:T(4,128)}), f32[4,4,1,4,128]{4,1,3,2,0:T(4,128)S(1)}, u32[]{:S(2)}, u32[]{:S(2)}) async-start(f32[4,4,1,4,128]{4,1,3,2,0:T(4,128)} %pad_maximum_fusion.11), calls=%async_computation.1 | async-start | bytes 65536 | tf_op jit(solution)/shard_map/all_to_all | solution.py:89
  27.4 6.8 %collective-permute-start.5 = (f32[256]{0:T(256)S(1)}, f32[256]{0:T(256)S(1)}, u32[]{:S(2)}, u32[]{:S(2)}) collective-permute-start(f32[256]{0:T(256)S(1)} %collective-permute-done.4), channel_id=1, source_target_pairs={{0,2},{1,3},{2,0},{3,1},{4,6},{5,7},{6,4},{7,5},{8,10},{9,11},{10,... | collective-permute-start | bytes 3080 | tf_op jit(solution)/shard_map/ppermute | solution.py:24
  30.3 3.9 %copy-start.5 = (f32[2,1,256]{2,1,0:T(1,128)}, f32[2,1,256]{2,1,0:T(1,128)S(1)}, u32[]{:S(2)}) copy-start(f32[2,1,256]{2,1,0:T(1,128)S(1)} %collective-permute-done.1) | copy-start | bytes 6148
  30.4 5.9 %collective-permute-start.3 = (f32[2,34,1]{2,1,0:T(8,128)S(1)}, f32[2,34,1]{2,1,0:T(8,128)S(1)}, u32[]{:S(2)}, u32[]{:S(2)}) collective-permute-start(f32[2,34,1]{2,1,0:T(8,128)S(1)} %get-tuple-element.17), channel_id=1, source_target_pairs={{0,1},{1,2},{2,3},{3,0},{4,5},{5,6},{6,7},{7,4},{8,9},{9,10},{10,1... | collective-permute-start | bytes 824 | tf_op jit(solution)/shard_map/ppermute | solution.py:15
  31.8 4.4 %collective-permute-start.2 = (f32[2,34,1]{2,1,0:T(8,128)S(1)}, f32[2,34,1]{2,1,0:T(8,128)S(1)}, u32[]{:S(2)}, u32[]{:S(2)}) collective-permute-start(f32[2,34,1]{2,1,0:T(8,128)S(1)} %get-tuple-element.16), channel_id=1, source_target_pairs={{1,0},{2,1},{3,2},{0,3},{5,4},{6,5},{7,6},{4,7},{9,8},{10,9},{11,1... | collective-permute-start | bytes 824 | tf_op jit(solution)/shard_map/ppermute | solution.py:18
  34.3 0.7 %slice-start = ((f32[2,1,256]{2,1,0:T(1,128)}), f32[1,1,256]{2,1,0:T(1,128)S(1)}, s32[]{:S(2)}) async-start(f32[2,1,256]{2,1,0:T(1,128)} %copy-done.5), calls=%async_computation.2 | async-start | bytes 2048 | tf_op jit(solution)/shard_map/slice | solution.py:78
  35.0 1.3 %copy-start.6 = (f32[2,1,256]{2,1,0:T(1,128)S(1)}, f32[2,1,256]{2,1,0:T(1,128)}, u32[]{:S(2)}) copy-start(f32[2,1,256]{2,1,0:T(1,128)} %copy-done.5) | copy-start | bytes 6148
